TPU v7x, 32 devices: a whole 2x2x4 slice. The times are simulated.
32 devices in a mesh: groups: 2 (over y), seq: 4 (over z), head: 2 (over x), layer: 2 (over core).
Axes of the slice: x: 2, y: 2, z: 4, core: 2. Of those that a mesh axis runs over, the one named last changes fastest.
Arguments:
- kv_cache: bfloat16 [2, 2, 8, 4096, 2, 128], P(None, 'layer', 'groups', 'seq', 'head'), parts along dimension 2, may hold values from -800 to 800
- valid_blocks: int32 [8], P('groups'), parts along dimension 0, may hold values from 1 to 32, 64 in all
Outputs:
- decode_cache: bfloat16 [2, 2, 8, 4096, 2, 128], P(None, 'layer', ('groups', 'seq'), None, 'head'), parts along dimension 2
- centers: float32 [2, 2, 8, 2, 128], P(None, 'layer', 'groups', 'head'), parts along dimension 2
- scales: float32 [2, 2, 8, 2, 128], P(None, 'layer', 'groups', 'head'), parts along dimension 2
There are 2 independent parts, one for each index of `groups`. A program takes and returns all parts, laid end to end along the dimension named above; each array names one. Nothing has to cross between parts.
Inputs may be any that keep to these rules, and one draw needn't show every extreme that they name: `valid_blocks`: the counts of the 4 users sum to 64, and the largest equals 32.
All inputs are finite; a program needn't handle non-finite values.
Results may differ from a plain program's by a relative error of at most 0.001.
Values may be sent and summed in bfloat16 or wider, within the bound.
A program may use at most 64 MiB of HBM per device.

v0:
```python
import jax
import jax.numpy as jnp
from jax import lax
from jax.sharding import PartitionSpec as P

BLOCK = 128
epsilon = 1e-06


def on_device(kv_cache, valid_blocks):
    kind_count, layer_dev, user_count, per_dev, heads_dev, head_dim = kv_cache.shape
    owners = lax.axis_size("seq")
    quarter = owners // user_count
    part_len = per_dev // quarter
    seq_index = lax.axis_index("seq")
    lengths = valid_blocks * BLOCK
    values = kv_cache.astype(jnp.float32)
    position = seq_index * per_dev + jnp.arange(per_dev, dtype=jnp.int32)
    is_live = position[None, :] < lengths[:, None]
    live_mask = is_live[None, None, :, :, None, None]
    local_sum = jnp.sum(jnp.where(live_mask, values, 0.0), axis=3)
    user_lengths = lengths.astype(jnp.float32)[None, None, :, None, None]
    totals = lax.psum(local_sum, "seq")
    centers = totals / user_lengths
    local_spread = jnp.max(
        jnp.where(live_mask, jnp.abs(values - centers[:, :, :, None]), 0.0), axis=3
    )
    spread = lax.pmax(local_spread, "seq")
    scales = spread + epsilon
    normed = jnp.where(
        live_mask, (values - centers[:, :, :, None]) / scales[:, :, :, None], 0.0
    ).astype(jnp.bfloat16)
    outgoing = normed.reshape(
        kind_count, layer_dev, user_count * quarter, part_len, heads_dev, head_dim
    )
    received = lax.all_to_all(outgoing, "seq", split_axis=2, concat_axis=2, tiled=True)
    arranged = received.reshape(kind_count, layer_dev, 1, owners * part_len, heads_dev, head_dim)
    return (arranged, centers, scales)


def solution(mesh):
    in_specs = (P(None, "layer", "groups", "seq", "head", None), P("groups"))
    out_specs = (
        P(None, "layer", ("groups", "seq"), None, "head", None),
        P(None, "layer", "groups", "head", None),
        P(None, "layer", "groups", "head", None),
    )
    return jax.shard_map(
        on_device, mesh=mesh, in_specs=in_specs, out_specs=out_specs, check_vma=False
    )
```

profile of v0, /device:TPU:0, one launch (start us, length us, event | category | flops | bytes accessed | tf_op | source)
XLA Modules:
  0.0 79.4 jit_solution(9776314781821777403)
XLA Ops:
  0.6 0.0 copy-start
  0.6 0.8 %fusion.7 = (f32[4]{0:T(128)S(1)}, s32[4]{0:T(128)S(1)}) fusion(s32[4]{0:T(128)} %param.3), kind=kLoop, calls=%fused_computation.14 | loop fusion | flops 8 | bytes 48 | tf_op jit(solution)/shard_map/convert_element_type | solution.py:22
  1.5 0.1 broadcast_compare_fusion
  1.5 2.8 %fusion.6 = f32[2,4,128]{2,0,1:T(2,128)S(1)} fusion(pred[4,1024]{1,0:T(4,128)(4,1)S(1)} %broadcast_compare_fusion, bf16[2,1,4,1024,1,128]{5,3,4,2,1,0:T(8,128)(2,1)} %param.2), kind=kLoop, calls=%fused_computation.8 | loop fusion | flops 3144704 | bytes 2105344 | tf_op jit(solution)/shard_map/reduce_sum | solution.py:21
  4.3 13.5 %psum.7 = f32[2,1,4,1,128]{4,0,2,3,1:T(2,128)S(1)} all-reduce(f32[2,1,4,1,128]{4,0,2,3,1:T(2,128)S(1)} %bitcast.10), channel_id=1, replica_groups=mesh['groups'=2,'seq'=4,'head'=2,'layer'=2] {'seq'}, use_global_device_ids=true, to_apply=%region_1.2 | all-reduce | flops 1024 | bytes 8192 | tf_op jit(solution)/shard_map/psum | solution.py:23
  17.8 0.1 fusion.9
  17.9 0.0 copy-done
  17.9 1.0 %fusion.3 = f32[2,4,128]{2,0,1:T(2,128)S(1)} fusion(f32[2,4,128]{2,0,1:T(2,128)S(1)} %fusion.9, pred[4,1024]{1,0:T(4,128)(4,1)S(1)} %broadcast_compare_fusion, bf16[2,1,4,1024,1,128]{5,3,4,2,1,0:T(8,128)(2,1)S(1)} %copy-done), kind=kLoop, calls=%fused_computation.5 | loop fusion | flops 5241856 | bytes 2109440 | tf_op jit(solution)/shard_map/reduce_max | solution.py:25
  18.9 8.4 %pmax.7 = f32[2,1,4,1,128]{4,0,2,3,1:T(2,128)S(1)} all-reduce(f32[2,1,4,1,128]{4,0,2,3,1:T(2,128)S(1)} %bitcast.11), channel_id=1, replica_groups=mesh['groups'=2,'seq'=4,'head'=2,'layer'=2] {'seq'}, use_global_device_ids=true, to_apply=%region_3.4 | all-reduce | flops 1024 | bytes 8192 | tf_op jit(solution)/shard_map/pmax | solution.py:28
  27.3 2.4 %fusion.5 = bf16[2,1,4,1024,1,128]{5,3,4,1,0,2:T(8,128)(2,1)} fusion(f32[2,4,128]{2,0,1:T(2,128)S(1)} %get-tuple-element.10, f32[2,4,128]{2,0,1:T(2,128)S(1)} %fusion.9, pred[4,1024]{1,0:T(4,128)(4,1)S(1)} %broadcast_compare_fusion, bf16[2,1,4,1024,1,128]{5,3,4,2,1,0:T(8,128)(2,1)S(1)} %copy-done), kind=kLoop, calls=%fused_computation.7 | loop fusion | flops 5242880 | bytes 4206592 | tf_op jit(solution)/shard_map/convert_element_type | solution.py:32
  29.7 3.6 %all-to-all-start = ((bf16[2,1,4,1024,1,128]{5,3,4,1,0,2:T(8,128)(2,1)}), bf16[2,1,4,1024,1,128]{5,3,4,1,0,2:T(8,128)(2,1)S(1)}, u32[]{:S(2)}, u32[]{:S(2)}) async-start(bf16[2,1,4,1024,1,128]{5,3,4,1,0,2:T(8,128)(2,1)} %fusion.5), calls=%async_computation | async-start | bytes 4194304 | tf_op jit(solution)/shard_map/all_to_all | solution.py:36
  33.3 0.1 broadcast_divide_fusion
  33.4 0.6 copy.16
  34.0 0.6 copy.17
  34.6 43.4 %all-to-all-done = bf16[2,1,4,1024,1,128]{5,3,4,1,0,2:T(8,128)(2,1)S(1)} async-done(((bf16[2,1,4,1024,1,128]{5,3,4,1,0,2:T(8,128)(2,1)}), bf16[2,1,4,1024,1,128]{5,3,4,1,0,2:T(8,128)(2,1)S(1)}, u32[]{:S(2)}, u32[]{:S(2)}) %all-to-all-start) | async-done | bytes 2097184 | tf_op jit(solution)/shard_map/all_to_all | solution.py:36
  77.9 1.5 %copy.14 = bf16[2,1,4,1024,1,128]{5,3,2,0,4,1:T(8,128)(2,1)} copy(bf16[2,1,4,1024,1,128]{5,3,4,1,0,2:T(8,128)(2,1)S(1)} %all-to-all-done) | data formatting | bytes 4194304 | tf_op jit(solution)/shard_map/all_to_all | solution.py:36
  (2 shorter events, 0.0 us)
Async XLA Ops:
  0.6 17.2 %copy-start = (bf16[2,1,4,1024,1,128]{5,3,4,2,1,0:T(8,128)(2,1)S(1)}, bf16[2,1,4,1024,1,128]{5,3,4,2,1,0:T(8,128)(2,1)}, u32[]{:S(2)}) copy-start(bf16[2,1,4,1024,1,128]{5,3,4,2,1,0:T(8,128)(2,1)} %param.2) | copy-start | bytes 6291460
  29.7 48.3 %all-to-all-start = ((bf16[2,1,4,1024,1,128]{5,3,4,1,0,2:T(8,128)(2,1)}), bf16[2,1,4,1024,1,128]{5,3,4,1,0,2:T(8,128)(2,1)S(1)}, u32[]{:S(2)}, u32[]{:S(2)}) async-start(bf16[2,1,4,1024,1,128]{5,3,4,1,0,2:T(8,128)(2,1)} %fusion.5), calls=%async_computation | async-start | bytes 4194304 | tf_op jit(solution)/shard_map/all_to_all | solution.py:36
where the time goes:
time: 79.7 us; the launch traced here: 79.4 us
  waiting for transfers between devices  43.4 us (54%)
  blocking collectives  21.9 us (27%)
  other arithmetic  7.21 us (9%)
  starting transfers between devices  3.61 us (5%)
  local copies, waits for them, and re-layouts  2.66 us (3%)
    all_to_all x1, waiting for transfers between devices, on_device(): lax.all_to_all(outgoing, 'seq', split_axis=2, concat_axis=2, tiled=True)  43.4 us
    psum x1, blocking collectives, on_device(): totals = lax.psum(local_sum, 'seq')  13.5 us
    pmax x1, blocking collectives, on_device(): spread = lax.pmax(local_spread, 'seq')  8.38 us
    all_to_all x1, starting transfers between devices, on_device(): lax.all_to_all(outgoing, 'seq', split_axis=2, concat_axis=2, tiled=True)  3.61 us
    reduce_sum x1, other arithmetic, on_device(): local_sum = jnp.sum(jnp.where(live_mask, values, 0.0), axis=3)  2.76 us
    convert_element_type x1, other arithmetic, on_device(): normed = jnp.where(live_mask, (values - centers[:, :, :, None]) / scales[...  2.37 us
  transfers between devices with their start and end apart: 1, of which 1 were waited for; matrix products, arithmetic and copies ran while one was open for 2% of the time, Pallas kernels for 0%

commit v1 on v0

--- a/solution.py
+++ b/solution.py
@@ -33,7 +33,10 @@
     outgoing = normed.reshape(
         kind_count, layer_dev, user_count * quarter, part_len, heads_dev, head_dim
     )
-    received = lax.all_to_all(outgoing, "seq", split_axis=2, concat_axis=2, tiled=True)
+    peers = lax.axis_size("seq")
+    parts = jnp.stack(jnp.split(outgoing, peers, axis=2), axis=0)
+    parts = lax.all_to_all(parts, "seq", split_axis=0, concat_axis=0)
+    received = jnp.concatenate(parts, axis=2)
     arranged = received.reshape(kind_count, layer_dev, 1, owners * part_len, heads_dev, head_dim)
     return (arranged, centers, scales)
 

time: 79.7 us -> 77.2 us (0.969)
  blocking collectives: 21.9 us -> 69.4 us
  waiting for transfers between devices: 43.4 us -> 0 us
  starting transfers between devices: 3.61 us -> 0 us
  other arithmetic: 7.21 us -> 5.24 us
  local copies, waits for them, and re-layouts: 2.66 us -> 1.61 us
    all_to_all x0 -> x1, blocking collectives: none -> 47.5 us  [on_device(): parts = lax.all_to_all(parts, 'seq', split_axis=0, concat_axis=0)]
    all_to_all x1 -> x0, waiting for transfers between devices: 43.4 us -> none  [on_device(): lax.all_to_all(outgoing, 'seq', split_axis=2, concat_axis=2, tiled=True)]
    all_to_all x1 -> x0, starting transfers between devices: 3.61 us -> none  [on_device(): lax.all_to_all(outgoing, 'seq', split_axis=2, concat_axis=2, tiled=True)]
    all_to_all x1 -> x0, local copies, waits for them, and re-layouts: 1.45 us -> none  [on_device(): lax.all_to_all(outgoing, 'seq', split_axis=2, concat_axis=2, tiled=True)]
    reshape x0 -> x1, local copies, waits for them, and re-layouts: none -> 1.45 us  [on_device(): received = jnp.concatenate(parts, axis=2)]
    convert_element_type x1, other arithmetic: 2.37 us -> 1.02 us  [on_device(): normed = jnp.where(live_mask, (values - centers[:, :, :, None]) / scales[...]
    unnamed x4 -> x6, local copies, waits for them, and re-layouts: 1.21 us -> 0.01 us
    reduce_sum x1, other arithmetic: 2.76 us -> 1.95 us  [on_device(): local_sum = jnp.sum(jnp.where(live_mask, values, 0.0), axis=3)]
  transfers between devices with their start and end apart: 1 -> 0, of which waited for: 1 -> 0; matrix products, arithmetic and copies ran while one was open for 2% -> 0% of each run, Pallas kernels for 0% -> 0%
where the time goes in v1:
time: 77.2 us; the launch traced here: 77 us
  blocking collectives  69.4 us (90%)
  other arithmetic  5.24 us (7%)
  local copies, waits for them, and re-layouts  1.61 us (2%)
    all_to_all x1, blocking collectives, on_device(): parts = lax.all_to_all(parts, 'seq', split_axis=0, concat_axis=0)  47.5 us
    psum x1, blocking collectives, on_device(): totals = lax.psum(local_sum, 'seq')  13.5 us
    pmax x1, blocking collectives, on_device(): spread = lax.pmax(local_spread, 'seq')  8.38 us
    reduce_sum x1, other arithmetic, on_device(): local_sum = jnp.sum(jnp.where(live_mask, values, 0.0), axis=3)  1.95 us

profile of v1, /device:TPU:0, one launch (start us, length us, event | category | flops | bytes accessed | tf_op | source)
XLA Modules:
  0.0 77.0 jit_solution(12210359469958879802)
XLA Ops:
  0.6 0.0 copy-start
  0.6 0.8 %fusion.7 = (f32[4]{0:T(128)S(1)}, s32[4]{0:T(128)S(1)}) fusion(s32[4]{0:T(128)} %param.3), kind=kLoop, calls=%fused_computation.19 | loop fusion | flops 8 | bytes 48 | tf_op jit(solution)/shard_map/convert_element_type | solution.py:22
  1.5 0.1 broadcast_compare_fusion
  1.5 1.9 %fusion.6 = f32[2,4,128]{2,1,0:T(4,128)S(1)} fusion(bf16[2,1,4,1024,1,128]{5,3,4,2,1,0:T(8,128)(2,1)} %param.2, pred[4,1024]{1,0:T(4,128)(4,1)S(1)} %broadcast_compare_fusion), kind=kLoop, calls=%fused_computation.8 | loop fusion | flops 3144704 | bytes 2105344 | tf_op jit(solution)/shard_map/reduce_sum | solution.py:21
  3.5 13.5 %psum.7 = f32[2,1,4,1,128]{4,3,2,1,0:T(1,128)S(1)} all-reduce(f32[2,1,4,1,128]{4,3,2,1,0:T(1,128)S(1)} %bitcast.25), channel_id=1, replica_groups=mesh['groups'=2,'seq'=4,'head'=2,'layer'=2] {'seq'}, use_global_device_ids=true, to_apply=%region_1.2 | all-reduce | flops 1024 | bytes 8192 | tf_op jit(solution)/shard_map/psum | solution.py:23
  17.0 0.1 broadcast_divide_fusion
  17.1 0.0 copy-start.1
  17.1 0.0 copy-done
  17.1 1.0 %fusion.3 = f32[2,4,128]{2,1,0:T(4,128)S(1)} fusion(bf16[2,1,4,1024,1,128]{5,3,4,2,1,0:T(8,128)(2,1)S(1)} %copy-done, f32[2,4,128]{2,1,0:T(4,128)S(1)} %bitcast.22, pred[4,1024]{1,0:T(4,128)(4,1)S(1)} %broadcast_compare_fusion), kind=kLoop, calls=%fused_computation.5 | loop fusion | flops 5241856 | bytes 2109440 | tf_op jit(solution)/shard_map/reduce_max | solution.py:25
  18.1 8.4 %pmax.7 = f32[2,1,4,1,128]{4,3,2,1,0:T(1,128)S(1)} all-reduce(f32[2,1,4,1,128]{4,3,2,1,0:T(1,128)S(1)} %bitcast.26), channel_id=1, replica_groups=mesh['groups'=2,'seq'=4,'head'=2,'layer'=2] {'seq'}, use_global_device_ids=true, to_apply=%region_3.4 | all-reduce | flops 1024 | bytes 8192 | tf_op jit(solution)/shard_map/pmax | solution.py:28
  26.5 0.0 copy-start.2
  26.5 1.0 %fusion.5 = bf16[2,1,4,1024,1,128]{5,3,4,2,1,0:T(8,128)(2,1)S(1)} fusion(bf16[2,1,4,1024,1,128]{5,3,4,2,1,0:T(8,128)(2,1)S(1)} %copy-done, f32[2,4,128]{2,1,0:T(4,128)S(1)} %bitcast.24, f32[2,4,128]{2,1,0:T(4,128)S(1)} %bitcast.23, pred[4,1024]{1,0:T(4,128)(4,1)S(1)} %broadcast_compare_fusion), kind=kLoop, calls=%fused_computation.7 | loop fusion | flops 5242880 | bytes 4206592 | tf_op jit(solution)/shard_map/convert_element_type | solution.py:32
  27.5 0.0 copy-done.1
  27.5 0.0 copy-done.2
  27.6 0.1 slice_bitcast_fusion.3
  27.7 0.3 pad_maximum_fusion
  28.0 47.5 %all_to_all.5 = bf16[4,2,1,1,1024,1,128]{6,4,1,5,3,2,0:T(8,128)(2,1)S(1)} all-to-all(bf16[4,2,1,1,1024,1,128]{6,4,1,5,3,2,0:T(8,128)(2,1)S(1)} %pad_maximum_fusion), channel_id=1, replica_groups=mesh['groups'=2,'seq'=4,'head'=2,'layer'=2] {'seq'}, dimensions={0} | all-to-all | bytes 4194304 | tf_op jit(solution)/shard_map/all_to_all | solution.py:38
  75.5 1.5 %copy.8 = bf16[2,1,4,1,1024,1,128]{6,4,2,0,5,3,1:T(8,128)(2,1)} copy(bf16[2,1,4,1,1024,1,128]{6,4,0,5,3,1,2:T(8,128)(2,1)S(1)} %bitcast.20) | data formatting | bytes 4194304 | tf_op jit(solution)/shard_map/reshape | solution.py:39
  (2 shorter events, 0.0 us)
Async XLA Ops:
  0.6 16.4 %copy-start = (bf16[2,1,4,1024,1,128]{5,3,4,2,1,0:T(8,128)(2,1)S(1)}, bf16[2,1,4,1024,1,128]{5,3,4,2,1,0:T(8,128)(2,1)}, u32[]{:S(2)}) copy-start(bf16[2,1,4,1024,1,128]{5,3,4,2,1,0:T(8,128)(2,1)} %param.2) | copy-start | bytes 6291460
  17.1 10.5 %copy-start.1 = (f32[2,1,4,1,128]{4,3,2,1,0:T(1,128)}, f32[2,1,4,1,128]{4,3,2,1,0:T(1,128)S(1)}, u32[]{:S(2)}) copy-start(f32[2,1,4,1,128]{4,3,2,1,0:T(1,128)S(1)} %broadcast_divide_fusion) | copy-start | bytes 12292
  26.5 1.0 %copy-start.2 = (f32[2,1,4,1,128]{4,3,2,1,0:T(1,128)}, f32[2,1,4,1,128]{4,3,2,1,0:T(1,128)S(1)}, u32[]{:S(2)}) copy-start(f32[2,1,4,1,128]{4,3,2,1,0:T(1,128)S(1)} %broadcast_add_fusion) | copy-start | bytes 12292
